TPU v7x, 32 devices: a whole 2x2x4 slice. The times are simulated.
32 devices in a mesh: row: 8 (over y, x, core), col: 4 (over z).
Axes of the slice: x: 2, y: 2, z: 4, core: 2. Of those that a mesh axis runs over, the one named last changes fastest.
Arguments:
- a_matrix: float32 [2048, 2048], P('row', 'col'), may hold values from -0.9 to 0.9
- b_matrix: float32 [2048, 2048], P('row', 'col'), may hold values from -0.9 to 0.9
- a_panel: float32 [2048, 1024], P('row', 'col'), may hold values from -0.9 to 0.9
- b_panel: float32 [2048, 1024], P('row', 'col'), may hold values from -0.9 to 0.9
Outputs:
- triangle: float32 [1024, 1024], P('row', 'col')
- pencil_cross: float32 [2048, 2048], P('row', 'col')
All inputs are finite; a program needn't handle non-finite values.
Results may differ from a plain program's by a relative error of at most 0.0003.
Values sent between devices are 32-bit elements; how exact they have to be, the bound alone decides.
No kernel may reach another device: no remote copies, remote signals or barrier semaphores. Data moves between devices by JAX's collectives and lax.ppermute only.
A program may use at most 64 MiB of HBM per device.

v0:
```python
import jax
import jax.numpy as jnp
from jax import lax
from jax.sharding import PartitionSpec as P

HIGHEST = lax.Precision.HIGHEST


def local(a_matrix, b_matrix, a_panel, b_panel):
    row_count = a_matrix.shape[0]
    panel_width = a_panel.shape[1]
    full_a, full_pa, full_pb = (
        lax.all_gather(a_matrix, "col", axis=1, tiled=True),
        lax.all_gather(a_panel, "col", axis=1, tiled=True),
        lax.all_gather(b_panel, "col", axis=1, tiled=True),
    )
    stacked = jnp.concatenate([full_pb, -full_pa], 0)
    own_block = jnp.concatenate([b_panel, -a_panel], 0)
    partial_gram = jnp.dot(own_block.T, stacked, precision=HIGHEST)
    gram_rows = lax.psum(partial_gram, "row")
    gram_matrix = lax.all_gather(gram_rows, "col", axis=0, tiled=True)
    lower_factor = jnp.linalg.cholesky(gram_matrix)
    q_rows = jax.scipy.linalg.solve_triangular(lower_factor, stacked.T, lower=True).T
    upper_rows = q_rows[:row_count]
    lower_rows = q_rows[row_count:]
    row_index = lax.axis_index("row")
    col_index = lax.axis_index("col")
    tri_rows = gram_matrix.shape[0] // lax.axis_size("row")
    corner = lax.dynamic_slice(
        lower_factor, (col_index * panel_width, row_index * tri_rows), (panel_width, tri_rows)
    )
    triangle = corner.T
    partial_z = jnp.dot(lower_rows.T, b_matrix, precision=HIGHEST)
    z_columns = lax.psum(partial_z, "row")
    v_block = jnp.dot(upper_rows, z_columns, precision=HIGHEST)
    pencil_cross = lax.psum_scatter(
        -jnp.dot(full_a.T, v_block, precision=HIGHEST), "row", scatter_dimension=0, tiled=True
    )
    return (triangle, pencil_cross)


def solution(mesh):
    in_specs = (P("row", "col"), P("row", "col"), P("row", "col"), P("row", "col"))
    out_specs = (P("row", "col"), P("row", "col"))
    return jax.shard_map(local, mesh=mesh, in_specs=in_specs, out_specs=out_specs, check_vma=False)
```

profile of v0, /device:TPU:0, one launch (start us, length us, event | category | flops | bytes accessed | tf_op | source)
XLA Modules:
  0.0 741.9 jit_solution(5404969723252647219)
XLA Ops:
  9.7 30.6 %all-gather.7.cloned.1.call-done = f32[256,1024]{1,0:T(8,128)} async-done(((f32[256,256]{1,0:T(8,128)}), f32[256,1024]{1,0:T(8,128)}) %all-gather.7.cloned.1.call-update) | async-done | bytes 1048592 | tf_op jit(solution)/shard_map/all_gather | solution.py:14
  41.6 27.7 %all-gather.5.cloned.1.call-done = f32[256,1024]{1,0:T(8,128)} async-done(((f32[256,256]{1,0:T(8,128)}), f32[256,1024]{1,0:T(8,128)}) %all-gather.5.cloned.1.call-update) | async-done | bytes 1048592 | tf_op jit(solution)/shard_map/all_gather | solution.py:15
  69.3 5.7 fusion.3
  75.1 56.2 %all-reduce.4.cloned.1.call-done = f32[256,1024]{0,1:T(8,128)} async-done(((f32[256,1024]{0,1:T(8,128)}), f32[256,1024]{0,1:T(8,128)}) %all-reduce.4.cloned.1.call-update) | async-done | bytes 1048592 | tf_op jit(solution)/shard_map/psum | solution.py:20
  132.9 79.8 %all-gather.9.cloned.1.call-done = f32[1024,1024]{0,1:T(8,128)} async-done(((f32[256,1024]{0,1:T(8,128)}), f32[1024,1024]{0,1:T(8,128)}) %all-gather.9.cloned.1.call-update) | async-done | bytes 4194320 | tf_op jit(solution)/shard_map/all_gather | solution.py:21
  212.7 5.5 copy.7
  218.2 4.4 fusion
  224.6 11.7 %cholesky.223 = f32[128,128]{1,0:T(8,128)S(1)} custom-call(f32[128,128]{1,0:T(8,128)S(1)} %cholesky.580), custom_call_target="Cholesky" | custom-call | tf_op jit(solution)/shard_map/jit(cholesky)/cholesky | solution.py:22
  238.8 9.8 %custom-call.63 = f32[1,128,128]{1,2,0:T(8,128)S(1)} custom-call(f32[1,128,128]{2,1,0:T(8,128)S(1)} %get-tuple-element.70), custom_call_target="InvertDiagBlocksLowerTriangular" | custom-call | tf_op jit(solution)/shard_map/jit(cholesky)/cholesky | solution.py:22
  252.6 11.9 %cholesky.244 = f32[128,128]{1,0:T(8,128)S(1)} custom-call(f32[128,128]{1,0:T(8,128)S(1)} %cholesky.584), custom_call_target="Cholesky" | custom-call | tf_op jit(solution)/shard_map/jit(cholesky)/cholesky | solution.py:22
  265.1 9.8 %custom-call.64 = f32[1,128,128]{1,2,0:T(8,128)S(1)} custom-call(f32[1,128,128]{2,1,0:T(8,128)S(1)} %get-tuple-element.67), custom_call_target="InvertDiagBlocksLowerTriangular" | custom-call | tf_op jit(solution)/shard_map/jit(cholesky)/cholesky | solution.py:22
  278.3 11.7 %cholesky.468 = f32[128,128]{1,0:T(8,128)S(1)} custom-call(f32[128,128]{1,0:T(8,128)S(1)} %cholesky.589), custom_call_target="Cholesky" | custom-call | tf_op jit(solution)/shard_map/jit(cholesky)/cholesky | solution.py:22
  290.7 9.8 %custom-call.65 = f32[1,128,128]{1,2,0:T(8,128)S(1)} custom-call(f32[1,128,128]{2,1,0:T(8,128)S(1)} %get-tuple-element.64), custom_call_target="InvertDiagBlocksLowerTriangular" | custom-call | tf_op jit(solution)/shard_map/jit(cholesky)/cholesky | solution.py:22
  304.0 12.1 %cholesky.487 = f32[128,128]{1,0:T(8,128)S(1)} custom-call(f32[128,128]{1,0:T(8,128)S(1)} %cholesky.594), custom_call_target="Cholesky" | custom-call | tf_op jit(solution)/shard_map/jit(cholesky)/cholesky | solution.py:22
  316.7 9.8 %custom-call.66 = f32[1,128,128]{1,2,0:T(8,128)S(1)} custom-call(f32[1,128,128]{2,1,0:T(8,128)S(1)} %get-tuple-element.61), custom_call_target="InvertDiagBlocksLowerTriangular" | custom-call | tf_op jit(solution)/shard_map/jit(cholesky)/cholesky | solution.py:22
  330.0 11.7 %cholesky.506 = f32[128,128]{1,0:T(8,128)S(1)} custom-call(f32[128,128]{1,0:T(8,128)S(1)} %cholesky.599), custom_call_target="Cholesky" | custom-call | tf_op jit(solution)/shard_map/jit(cholesky)/cholesky | solution.py:22
  342.4 10.0 %custom-call.67 = f32[1,128,128]{1,2,0:T(8,128)S(1)} custom-call(f32[1,128,128]{2,1,0:T(8,128)S(1)} %get-tuple-element.58), custom_call_target="InvertDiagBlocksLowerTriangular" | custom-call | tf_op jit(solution)/shard_map/jit(cholesky)/cholesky | solution.py:22
  355.6 11.7 %cholesky.526 = f32[128,128]{1,0:T(8,128)S(1)} custom-call(f32[128,128]{1,0:T(8,128)S(1)} %cholesky.604), custom_call_target="Cholesky" | custom-call | tf_op jit(solution)/shard_map/jit(cholesky)/cholesky | solution.py:22
  368.0 9.8 %custom-call.68 = f32[1,128,128]{1,2,0:T(8,128)S(1)} custom-call(f32[1,128,128]{2,1,0:T(8,128)S(1)} %get-tuple-element.55), custom_call_target="InvertDiagBlocksLowerTriangular" | custom-call | tf_op jit(solution)/shard_map/jit(cholesky)/cholesky | solution.py:22
  380.8 11.7 %cholesky.546 = f32[128,128]{1,0:T(8,128)S(1)} custom-call(f32[128,128]{1,0:T(8,128)S(1)} %cholesky.609), custom_call_target="Cholesky" | custom-call | tf_op jit(solution)/shard_map/jit(cholesky)/cholesky | solution.py:22
  393.2 9.8 %custom-call.69 = f32[1,128,128]{1,2,0:T(8,128)S(1)} custom-call(f32[1,128,128]{2,1,0:T(8,128)S(1)} %get-tuple-element.52), custom_call_target="InvertDiagBlocksLowerTriangular" | custom-call | tf_op jit(solution)/shard_map/jit(cholesky)/cholesky | solution.py:22
  405.6 11.7 %cholesky.564 = f32[128,128]{1,0:T(8,128)S(1)} custom-call(f32[128,128]{1,0:T(8,128)S(1)} %convolution_subtract_fusion.13), custom_call_target="Cholesky" | custom-call | tf_op jit(solution)/shard_map/jit(cholesky)/cholesky | solution.py:22
  427.6 6.8 fusion.1
  434.3 27.5 %while.1 = (s32[]{:T(128)}, f32[1024,1024]{1,0:T(8,128)}, s32[8,2]{0,1:T(2,128)S(1)}, f32[8,128,128]{2,1,0:T(8,128)}, s32[]{:T(128)}) while((s32[]{:T(128)}, f32[1024,1024]{1,0:T(8,128)}, s32[8,2]{0,1:T(2,128)S(1)}, f32[8,128,128]{2,1,0:T(8,128)}, s32[]{:T(128)}) %tuple.63), condition=%wide.while_cond, body=%wide.while_body.sunk | while | flops 2 | bytes 132205 | solution.py:23
  461.8 79.8 %custom-call.70 = f32[8,128,128]{1,2,0:T(8,128)S(1)} custom-call(f32[8,128,128]{2,1,0:T(8,128)} %get-tuple-element.9), custom_call_target="InvertDiagBlocksLowerTriangular" | custom-call | tf_op jit(solution)/shard_map/jit(_solve_triangular)/triangular_solve | solution.py:23
  556.2 3.6 convolution_subtract_fusion.7
  560.3 4.3 convolution_subtract_fusion.3
  570.1 59.8 %all-reduce.6.cloned.1.call-done = f32[1024,512]{1,0:T(8,128)} async-done(((f32[1024,512]{1,0:T(8,128)}), f32[1024,512]{1,0:T(8,128)}) %all-reduce.6.cloned.1.call-update) | async-done | bytes 2097168 | tf_op jit(solution)/shard_map/psum | solution.py:34
  629.8 3.5 fusion.6
  633.4 42.7 %all-gather.11.cloned.1.call-done = f32[256,2048]{1,0:T(8,128)} async-done(((f32[256,512]{1,0:T(8,128)}), f32[256,2048]{1,0:T(8,128)}) %all-gather.11.cloned.1.call-update) | async-done | bytes 2097168 | tf_op jit(solution)/shard_map/all_gather | solution.py:13
  676.0 6.7 negate_bitcast_fusion
  684.5 48.3 %reduce-scatter.2.cloned.1.call-done = f32[256,512]{0,1:T(8,128)} async-done(((f32[2048,512]{0,1:T(8,128)}), f32[256,512]{0,1:T(8,128)}) %reduce-scatter.2.cloned.1.call-update) | async-done | bytes 524304 | tf_op jit(solution)/shard_map/reduce_scatter | solution.py:36
  (112 shorter events, 93.8 us)
Async XLA Ops:
  7.2 559.1 %copy-start = (f32[256,512]{1,0:T(8,128)S(1)}, f32[256,512]{1,0:T(8,128)}, u32[]{:S(2)}) copy-start(f32[256,512]{1,0:T(8,128)} %param.5) | copy-start | bytes 1572868
  7.2 62.1 %copy-start.6 = (f32[256,256]{1,0:T(8,128)S(1)}, f32[256,256]{1,0:T(8,128)}, u32[]{:S(2)}) copy-start(f32[256,256]{1,0:T(8,128)} %param.7) | copy-start | bytes 786436
  7.2 33.1 %all-gather.7.cloned.1.call-start = ((), (), s32[]{:S(2)}) async-start(), calls=%async_computation.2 | async-start | bytes 1310720 | tf_op jit(solution)/shard_map/all_gather | solution.py:14
  7.9 61.3 %all-gather.5.cloned.1.call-start = ((), (), s32[]{:S(2)}) async-start(), calls=%async_computation.1 | async-start | bytes 1310720 | tf_op jit(solution)/shard_map/all_gather | solution.py:15
  8.7 122.6 %all-reduce.4.cloned.1.call-start = ((), (), s32[]{:S(2)}) async-start(), calls=%async_computation.3 | async-start | bytes 2097152 | tf_op jit(solution)/shard_map/psum | solution.py:20
  69.3 62.1 %copy-start.3 = (f32[256,1024]{1,0:T(8,128)S(1)}, f32[256,1024]{1,0:T(8,128)}, u32[]{:S(2)}) copy-start(f32[256,1024]{1,0:T(8,128)} %all-gather.5.cloned.1.call-done) | copy-start | bytes 3145732
  75.0 137.7 %all-gather.9.cloned.1.call-start = ((), (), s32[]{:S(2)}) async-start(), calls=%async_computation.4 | async-start | bytes 5242880 | tf_op jit(solution)/shard_map/all_gather | solution.py:21
  131.3 498.5 %all-reduce.6.cloned.1.call-start = ((), (), s32[]{:S(2)}) async-start(), calls=%async_computation.5 | async-start | bytes 4194304 | tf_op jit(solution)/shard_map/psum | solution.py:34
  222.7 1.9 copy-start.1
  427.6 114.1 %copy-start.2 = (f32[1024,512]{0,1:T(8,128)S(1)}, f32[1024,512]{0,1:T(8,128)}, u32[]{:S(2)}) copy-start(f32[1024,512]{0,1:T(8,128)} %fusion.2) | copy-start | bytes 6291460
  565.0 1.3 copy-start.4
  569.4 60.4 %copy-start.5 = (f32[1024,512]{1,0:T(8,128)S(1)}, f32[1024,512]{1,0:T(8,128)}, u32[]{:S(2)}) copy-start(f32[1024,512]{1,0:T(8,128)} %copy-done.4) | copy-start | bytes 6291460
  569.4 106.6 %all-gather.11.cloned.1.call-start = ((), (), s32[]{:S(2)}) async-start(), calls=%async_computation.6 | async-start | bytes 2621440 | tf_op jit(solution)/shard_map/all_gather | solution.py:13
  570.0 162.8 %reduce-scatter.2.cloned.1.call-start = ((), (), s32[]{:S(2)}) async-start(), calls=%async_computation.7 | async-start | bytes 4718592 | tf_op jit(solution)/shard_map/reduce_scatter | solution.py:36
Sparse Core Ops, SparseCore 0:
  9.6 30.6 all-gather.6
  41.9 27.3 all-gather.4
  75.2 56.0 all-reduce.3
  132.7 79.9 all-gather.8
  569.6 60.2 all-reduce.5
  631.3 44.7 all-gather.10
  682.9 49.8 reduce-scatter.1
where the time goes:
time: 747 us; the launch traced here: 742 us
  waiting for transfers between devices  347 us (46%)
  other arithmetic  267 us (36%)
  matrix products  65.4 us (9%)
  local copies, waits for them, and re-layouts  42.5 us (6%)
  between operations  19.6 us (3%)
    another operation x30, other arithmetic, local(): lower_factor = jnp.linalg.cholesky(gram_matrix)  172 us
    another operation x3, other arithmetic, local(): jax.scipy.linalg.solve_triangular(lower_factor, stacked.T, lower=True)  86.6 us
    all_gather x1, waiting for transfers between devices, local(): gram_matrix = lax.all_gather(gram_rows, 'col', axis=0, tiled=True)  79.8 us
    psum x1, waiting for transfers between devices, local(): z_columns = lax.psum(partial_z, 'row')  59.8 us
    psum x1, waiting for transfers between devices, local(): gram_rows = lax.psum(partial_gram, 'row')  56.2 us
    reduce_scatter x1, waiting for transfers between devices, local(): lax.psum_scatter(-jnp.dot(full_a.T, v_block, precision=HIGHEST), 'row', s...  48.3 us
    all_gather x1, waiting for transfers between devices, local(): lax.all_gather(a_matrix, 'col', axis=1, tiled=True)  42.7 us
    all_gather x1, waiting for transfers between devices, local(): lax.all_gather(a_panel, 'col', axis=1, tiled=True)  30.6 us
  transfers between devices with their start and end apart: 7, of which 7 were waited for; matrix products, arithmetic and copies ran while one was open for 1% of the time, Pallas kernels for 0%

commit v1 on v0

--- a/solution.py
+++ b/solution.py
@@ -1,3 +1,4 @@
+import functools
 import jax
 import jax.numpy as jnp
 from jax import lax
@@ -6,11 +7,38 @@
 HIGHEST = lax.Precision.HIGHEST
 
 
+def deliver_samples(row_data, array_axis):
+    answer, t1, ready = (lax.axis_size("col"), lax.axis_index("col"), row_data.shape[array_axis])
+    tray = [(dev_j, (dev_j + 1) % answer) for dev_j in range(answer)]
+    pile = [(dev_j, (dev_j - 1) % answer) for dev_j in range(answer)]
+    h_now = jnp.zeros(
+        (*row_data.shape[:array_axis], answer * ready, *row_data.shape[array_axis + 1 :]),
+        row_data.dtype,
+    )
+    h_now = lax.dynamic_update_slice_in_dim(h_now, row_data, t1 * ready, axis=array_axis)
+    upper = f_next = row_data
+    arr_out = answer // 2
+    for k in range(1, arr_out + 1):
+        upper = lax.ppermute(upper, "col", tray)
+        h_now = lax.dynamic_update_slice_in_dim(
+            h_now, upper, (t1 - k) % answer * ready, axis=array_axis
+        )
+        if k < answer - arr_out:
+            f_next = lax.ppermute(f_next, "col", pile)
+            h_now = lax.dynamic_update_slice_in_dim(
+                h_now, f_next, (t1 + k) % answer * ready, axis=array_axis
+            )
+    return h_now
+
+
+flows_supply = functools.partial(deliver_samples, array_axis=1)
+
+
 def local(a_matrix, b_matrix, a_panel, b_panel):
     row_count = a_matrix.shape[0]
     panel_width = a_panel.shape[1]
     full_a, full_pa, full_pb = (
-        lax.all_gather(a_matrix, "col", axis=1, tiled=True),
+        flows_supply(a_matrix),
         lax.all_gather(a_panel, "col", axis=1, tiled=True),
         lax.all_gather(b_panel, "col", axis=1, tiled=True),
     )

time: 747 us -> 702 us (0.940)
  waiting for transfers between devices: 347 us -> 298 us
    all_gather x1 -> x0, waiting for transfers between devices: 42.7 us -> none  [local(): lax.all_gather(a_matrix, 'col', axis=1, tiled=True)]
    psum x1, waiting for transfers between devices: 59.8 us -> 32 us  [local(): z_columns = lax.psum(partial_z, 'row')]
    ppermute x0 -> x3, waiting for transfers between devices: none -> 21.6 us  [the longest x1 21.6 us: deliver_samples(): f_next = lax.ppermute(f_next, 'col', pile)]
  transfers between devices with their start and end apart: 7 -> 9, of which waited for: 7 -> 7; matrix products, arithmetic and copies ran while one was open for 1% -> 51% of each run, Pallas kernels for 0% -> 0%
where the time goes in v1:
time: 702 us; the launch traced here: 697 us
  waiting for transfers between devices  298 us (42%)
  other arithmetic  267 us (38%)
  matrix products  64.2 us (9%)
  local copies, waits for them, and re-layouts  44.1 us (6%)
  between operations  19.7 us (3%)
    another operation x30, other arithmetic, local(): lower_factor = jnp.linalg.cholesky(gram_matrix)  172 us
    another operation x3, other arithmetic, local(): jax.scipy.linalg.solve_triangular(lower_factor, stacked.T, lower=True)  86.6 us
    all_gather x1, waiting for transfers between devices, local(): gram_matrix = lax.all_gather(gram_rows, 'col', axis=0, tiled=True)  80.1 us
    psum x1, waiting for transfers between devices, local(): gram_rows = lax.psum(partial_gram, 'row')  56.2 us
    reduce_scatter x1, waiting for transfers between devices, local(): lax.psum_scatter(-jnp.dot(full_a.T, v_block, precision=HIGHEST), 'row', s...  48.7 us
    psum x1, waiting for transfers between devices, local(): z_columns = lax.psum(partial_z, 'row')  32 us
    all_gather x1, waiting for transfers between devices, local(): lax.all_gather(a_panel, 'col', axis=1, tiled=True)  30.6 us
    all_gather x1, waiting for transfers between devices, local(): lax.all_gather(b_panel, 'col', axis=1, tiled=True)  27.7 us
  transfers between devices with their start and end apart: 9, of which 7 were waited for; matrix products, arithmetic and copies ran while one was open for 51% of the time, Pallas kernels for 0%

profile of v1, /device:TPU:0, one launch (start us, length us, event | category | flops | bytes accessed | tf_op | source)
XLA Modules:
  0.0 697.3 jit_solution(10578782999233248892)
XLA Ops:
  9.7 30.6 %all-gather.6.cloned.1.call-done = f32[256,1024]{1,0:T(8,128)} async-done(((f32[256,256]{1,0:T(8,128)}), f32[256,1024]{1,0:T(8,128)}) %all-gather.6.cloned.1.call-update) | async-done | bytes 1048592 | tf_op jit(solution)/shard_map/all_gather | solution.py:42
  41.6 27.7 %all-gather.4.cloned.1.call-done = f32[256,1024]{1,0:T(8,128)} async-done(((f32[256,256]{1,0:T(8,128)}), f32[256,1024]{1,0:T(8,128)}) %all-gather.4.cloned.1.call-update) | async-done | bytes 1048592 | tf_op jit(solution)/shard_map/all_gather | solution.py:43
  69.3 5.7 fusion.3
  75.1 56.2 %all-reduce.4.cloned.1.call-done = f32[256,1024]{0,1:T(8,128)} async-done(((f32[256,1024]{0,1:T(8,128)}), f32[256,1024]{0,1:T(8,128)}) %all-reduce.4.cloned.1.call-update) | async-done | bytes 1048592 | tf_op jit(solution)/shard_map/psum | solution.py:48
  134.3 80.1 %all-gather.8.cloned.1.call-done = f32[1024,1024]{0,1:T(8,128)} async-done(((f32[256,1024]{0,1:T(8,128)}), f32[1024,1024]{0,1:T(8,128)}) %all-gather.8.cloned.1.call-update) | async-done | bytes 4194320 | tf_op jit(solution)/shard_map/all_gather | solution.py:49
  214.4 5.5 copy.7
  219.9 4.4 fusion
  226.3 11.7 %cholesky.223 = f32[128,128]{1,0:T(8,128)S(1)} custom-call(f32[128,128]{1,0:T(8,128)S(1)} %cholesky.580), custom_call_target="Cholesky" | custom-call | tf_op jit(solution)/shard_map/jit(cholesky)/cholesky | solution.py:50
  238.1 9.8 %custom-call.63 = f32[1,128,128]{1,2,0:T(8,128)S(1)} custom-call(f32[1,128,128]{2,1,0:T(8,128)S(1)} %get-tuple-element.70), custom_call_target="InvertDiagBlocksLowerTriangular" | custom-call | tf_op jit(solution)/shard_map/jit(cholesky)/cholesky | solution.py:50
  254.3 11.9 %cholesky.244 = f32[128,128]{1,0:T(8,128)S(1)} custom-call(f32[128,128]{1,0:T(8,128)S(1)} %cholesky.584), custom_call_target="Cholesky" | custom-call | tf_op jit(solution)/shard_map/jit(cholesky)/cholesky | solution.py:50
  266.8 9.8 %custom-call.64 = f32[1,128,128]{1,2,0:T(8,128)S(1)} custom-call(f32[1,128,128]{2,1,0:T(8,128)S(1)} %get-tuple-element.67), custom_call_target="InvertDiagBlocksLowerTriangular" | custom-call | tf_op jit(solution)/shard_map/jit(cholesky)/cholesky | solution.py:50
  280.0 11.7 %cholesky.468 = f32[128,128]{1,0:T(8,128)S(1)} custom-call(f32[128,128]{1,0:T(8,128)S(1)} %cholesky.589), custom_call_target="Cholesky" | custom-call | tf_op jit(solution)/shard_map/jit(cholesky)/cholesky | solution.py:50
  293.0 9.8 %custom-call.65 = f32[1,128,128]{1,2,0:T(8,128)S(1)} custom-call(f32[1,128,128]{2,1,0:T(8,128)S(1)} %get-tuple-element.64), custom_call_target="InvertDiagBlocksLowerTriangular" | custom-call | tf_op jit(solution)/shard_map/jit(cholesky)/cholesky | solution.py:50
  306.4 12.1 %cholesky.487 = f32[128,128]{1,0:T(8,128)S(1)} custom-call(f32[128,128]{1,0:T(8,128)S(1)} %cholesky.594), custom_call_target="Cholesky" | custom-call | tf_op jit(solution)/shard_map/jit(cholesky)/cholesky | solution.py:50
  319.8 9.8 %custom-call.66 = f32[1,128,128]{1,2,0:T(8,128)S(1)} custom-call(f32[1,128,128]{2,1,0:T(8,128)S(1)} %get-tuple-element.61), custom_call_target="InvertDiagBlocksLowerTriangular" | custom-call | tf_op jit(solution)/shard_map/jit(cholesky)/cholesky | solution.py:50
  333.0 11.7 %cholesky.506 = f32[128,128]{1,0:T(8,128)S(1)} custom-call(f32[128,128]{1,0:T(8,128)S(1)} %cholesky.599), custom_call_target="Cholesky" | custom-call | tf_op jit(solution)/shard_map/jit(cholesky)/cholesky | solution.py:50
  346.1 9.9 %custom-call.67 = f32[1,128,128]{1,2,0:T(8,128)S(1)} custom-call(f32[1,128,128]{2,1,0:T(8,128)S(1)} %get-tuple-element.58), custom_call_target="InvertDiagBlocksLowerTriangular" | custom-call | tf_op jit(solution)/shard_map/jit(cholesky)/cholesky | solution.py:50
  359.4 11.7 %cholesky.526 = f32[128,128]{1,0:T(8,128)S(1)} custom-call(f32[128,128]{1,0:T(8,128)S(1)} %cholesky.604), custom_call_target="Cholesky" | custom-call | tf_op jit(solution)/shard_map/jit(cholesky)/cholesky | solution.py:50
  372.4 9.8 %custom-call.68 = f32[1,128,128]{1,2,0:T(8,128)S(1)} custom-call(f32[1,128,128]{2,1,0:T(8,128)S(1)} %get-tuple-element.55), custom_call_target="InvertDiagBlocksLowerTriangular" | custom-call | tf_op jit(solution)/shard_map/jit(cholesky)/cholesky | solution.py:50
  385.2 11.9 %cholesky.546 = f32[128,128]{1,0:T(8,128)S(1)} custom-call(f32[128,128]{1,0:T(8,128)S(1)} %cholesky.609), custom_call_target="Cholesky" | custom-call | tf_op jit(solution)/shard_map/jit(cholesky)/cholesky | solution.py:50
  398.3 9.8 %custom-call.69 = f32[1,128,128]{1,2,0:T(8,128)S(1)} custom-call(f32[1,128,128]{2,1,0:T(8,128)S(1)} %get-tuple-element.52), custom_call_target="InvertDiagBlocksLowerTriangular" | custom-call | tf_op jit(solution)/shard_map/jit(cholesky)/cholesky | solution.py:50
  410.8 11.7 %cholesky.564 = f32[128,128]{1,0:T(8,128)S(1)} custom-call(f32[128,128]{1,0:T(8,128)S(1)} %convolution_subtract_fusion.13), custom_call_target="Cholesky" | custom-call | tf_op jit(solution)/shard_map/jit(cholesky)/cholesky | solution.py:50
  429.5 6.8 fusion.1
  436.2 27.5 %while.1 = (s32[]{:T(128)}, f32[1024,1024]{1,0:T(8,128)}, s32[8,2]{0,1:T(2,128)S(1)}, f32[8,128,128]{2,1,0:T(8,128)}, s32[]{:T(128)}) while((s32[]{:T(128)}, f32[1024,1024]{1,0:T(8,128)}, s32[8,2]{0,1:T(2,128)S(1)}, f32[8,128,128]{2,1,0:T(8,128)}, s32[]{:T(128)}) %tuple.63), condition=%wide.while_cond, body=%wide.while_body.sunk | while | flops 2 | bytes 132205 | solution.py:51
  463.7 79.8 %custom-call.70 = f32[8,128,128]{1,2,0:T(8,128)S(1)} custom-call(f32[8,128,128]{2,1,0:T(8,128)} %get-tuple-element.9), custom_call_target="InvertDiagBlocksLowerTriangular" | custom-call | tf_op jit(solution)/shard_map/jit(_solve_triangular)/triangular_solve | solution.py:51
  558.1 3.6 convolution_subtract_fusion.7
  562.2 4.3 convolution_subtract_fusion.3
  575.1 21.6 %collective-permute-done.1 = f32[256,512]{1,0:T(8,128)} collective-permute-done((f32[256,512]{1,0:T(8,128)S(1)}, f32[256,512]{1,0:T(8,128)}, u32[]{:S(2)}, u32[]{:S(2)}) %collective-permute-start.1) | collective-permute-done | bytes 524320 | tf_op jit(solution)/shard_map/ppermute | solution.py:27
  598.9 32.0 %all-reduce.6.cloned.1.call-done = f32[1024,512]{1,0:T(8,128)} async-done(((f32[1024,512]{1,0:T(8,128)}), f32[1024,512]{1,0:T(8,128)}) %all-reduce.6.cloned.1.call-update) | async-done | bytes 2097168 | tf_op jit(solution)/shard_map/psum | solution.py:62
  631.0 3.8 fusion.6
  634.8 5.1 convolution_negate_fusion
  641.6 48.7 %reduce-scatter.2.cloned.1.call-done = f32[256,512]{1,0:T(8,128)} async-done(((f32[2048,512]{1,0:T(8,128)}), f32[256,512]{1,0:T(8,128)}) %reduce-scatter.2.cloned.1.call-update) | async-done | bytes 524304 | tf_op jit(solution)/shard_map/reduce_scatter | solution.py:64
  (119 shorter events, 98.5 us)
Async XLA Ops:
  7.2 561.0 %copy-start = (f32[256,512]{1,0:T(8,128)S(1)}, f32[256,512]{1,0:T(8,128)}, u32[]{:S(2)}) copy-start(f32[256,512]{1,0:T(8,128)} %param.5) | copy-start | bytes 1572868
  7.2 62.1 %copy-start.5 = (f32[256,256]{1,0:T(8,128)S(1)}, f32[256,256]{1,0:T(8,128)}, u32[]{:S(2)}) copy-start(f32[256,256]{1,0:T(8,128)} %param.7) | copy-start | bytes 786436
  7.2 33.1 %all-gather.6.cloned.1.call-start = ((), (), s32[]{:S(2)}) async-start(), calls=%async_computation.2 | async-start | bytes 1310720 | tf_op jit(solution)/shard_map/all_gather | solution.py:42
  7.9 61.3 %all-gather.4.cloned.1.call-start = ((), (), s32[]{:S(2)}) async-start(), calls=%async_computation.1 | async-start | bytes 1310720 | tf_op jit(solution)/shard_map/all_gather | solution.py:43
  8.7 122.6 %all-reduce.4.cloned.1.call-start = ((), (), s32[]{:S(2)}) async-start(), calls=%async_computation.3 | async-start | bytes 2097152 | tf_op jit(solution)/shard_map/psum | solution.py:48
  69.3 63.6 %copy-start.3 = (f32[256,1024]{1,0:T(8,128)S(1)}, f32[256,1024]{1,0:T(8,128)}, u32[]{:S(2)}) copy-start(f32[256,1024]{1,0:T(8,128)} %all-gather.4.cloned.1.call-done) | copy-start | bytes 3145732
  75.0 139.4 %all-gather.8.cloned.1.call-start = ((), (), s32[]{:S(2)}) async-start(), calls=%async_computation.4 | async-start | bytes 5242880 | tf_op jit(solution)/shard_map/all_gather | solution.py:49
  131.3 499.7 %all-reduce.6.cloned.1.call-start = ((), (), s32[]{:S(2)}) async-start(), calls=%async_computation.5 | async-start | bytes 4194304 | tf_op jit(solution)/shard_map/psum | solution.py:62
  131.3 441.6 %collective-permute-start = (f32[256,512]{1,0:T(8,128)}, f32[256,512]{1,0:T(8,128)}, u32[]{:S(2)}, u32[]{:S(2)}) collective-permute-start(f32[256,512]{1,0:T(8,128)} %param.4), channel_id=1, source_target_pairs={{0,1},{1,2},{2,3},{3,0},{4,5},{5,6},{6,7},{7,4},{8,9},{9,10},{10,1... | collective-permute-start | bytes 1572872 | tf_op jit(solution)/shard_map/ppermute | solution.py:22
  224.4 1.9 copy-start.1
  429.5 114.1 %copy-start.2 = (f32[1024,512]{0,1:T(8,128)S(1)}, f32[1024,512]{0,1:T(8,128)}, u32[]{:S(2)}) copy-start(f32[1024,512]{0,1:T(8,128)} %fusion.2) | copy-start | bytes 6291460
  566.9 1.3 copy-start.4
  568.2 3.3 copy-start.6
  571.4 118.9 %reduce-scatter.2.cloned.1.call-start = ((), (), s32[]{:S(2)}) async-start(), calls=%async_computation.6 | async-start | bytes 4718592 | tf_op jit(solution)/shard_map/reduce_scatter | solution.py:64
  571.5 25.2 %collective-permute-start.1 = (f32[256,512]{1,0:T(8,128)S(1)}, f32[256,512]{1,0:T(8,128)}, u32[]{:S(2)}, u32[]{:S(2)}) collective-permute-start(f32[256,512]{1,0:T(8,128)S(1)} %copy-done.6), channel_id=1, source_target_pairs={{0,3},{1,0},{2,1},{3,2},{4,7},{5,4},{6,5},{7,6},{8,11},{9,8},{10,9... | collective-permute-start | bytes 1572872 | tf_op jit(solution)/shard_map/ppermute | solution.py:27
  573.0 24.8 %collective-permute-start.2 = (f32[256,512]{1,0:T(8,128)}, f32[256,512]{1,0:T(8,128)}, u32[]{:S(2)}, u32[]{:S(2)}) collective-permute-start(f32[256,512]{1,0:T(8,128)} %collective-permute-done), channel_id=1, source_target_pairs={{0,1},{1,2},{2,3},{3,0},{4,5},{5,6},{6,7},{7,4},{8,9},{9,10},{10,1... | collective-permute-start | bytes 1572872 | tf_op jit(solution)/shard_map/ppermute | solution.py:22
Sparse Core Ops, SparseCore 0:
  9.6 30.6 all-gather.5
  41.9 27.3 all-gather.3
  75.2 56.0 all-reduce.3
  132.7 81.6 all-gather.7
  571.6 59.3 all-reduce.5
  640.0 50.2 reduce-scatter.1
